TPU v7x, 128 devices: a whole 4x4x4 slice. The times are simulated.
128 devices in a mesh: circ: 32 (over x_hi, y, z), side: 4 (over x_lo, core).
Axes of the slice: x: 4 (x_hi: 2, x_lo: 2; x = x_hi * 2 + x_lo), y: 4, z: 4, core: 2. Of those that a mesh axis runs over, the one named last changes fastest.
Arguments:
- field: float32 [4, 7, 7, 7, 8, 4096], P('side', None, None, None, None, 'circ'), may hold values from -6 to 6
- coeffs: float32 [4, 3, 7, 7, 7, 8, 4096], P('side', None, None, None, None, None, 'circ'), may hold values from 0.25 to 1.5
- reaction: float32 [4, 7, 7, 7, 8, 4096], P('side', None, None, None, None, 'circ'), may hold values from 0.25 to 8
- step_scale: float32 [4, 7, 7, 7, 8, 4096], P('side', None, None, None, None, 'circ'), may hold values from 0.0001 to 0.0003
- rotation: int32 [4], replicated, may hold values from 0 to 12287
Outputs:
- advanced: float32 [4, 7, 7, 7, 8, 4096], P('side', None, None, None, None, 'circ')
Inputs may be any that keep to these rules, and one draw needn't show every extreme that they name: `rotation`: rotor position in units of one 3-th of an element's circumferential width.
All inputs are finite; a program needn't handle non-finite values.
Results may differ from a plain program's by a relative error of at most 0.0001.
Values sent between devices are 32-bit elements; how exact they have to be, the bound alone decides.
No kernel may reach another device: no remote copies, remote signals or barrier semaphores. Data moves between devices by JAX's collectives and lax.ppermute only.
A program may use at most 128 MiB of HBM per device.

v0:
```python
from typing import NamedTuple

import jax
import jax.numpy as jnp
import numpy as np
from jax import lax
from jax.experimental import pallas as pl
from jax.experimental.pallas import tpu as pltpu
from jax.sharding import PartitionSpec as P

SUBSTEPS = 3
STEPS = 4
N = 7
CIRC = 32
SIDES = 4
VMEM_LIMIT = 16 * 2**20
AXES = ("circ", "side")


def gll_points():
    return np.array(
        [
            -1.0,
            -0.830223896278567,
            -0.4688487934707142,
            0.0,
            0.4688487934707142,
            0.830223896278567,
            1.0,
        ]
    )


def derivative_table():
    points = gll_points()
    weights = np.array(
        [1.0 / np.prod([points[j] - points[k] for k in range(N) if k != j]) for j in range(N)]
    )
    derivative = np.zeros((N, N))
    for i in range(N):
        for j in range(N):
            if i != j:
                derivative[i, j] = weights[j] / weights[i] / (points[i] - points[j])
        derivative[i, i] = -np.sum(derivative[i])
    return derivative


def mortar_table(substep):
    points = gll_points()
    heights = (1.0 + points) * 0.5
    fraction = substep / SUBSTEPS
    on_right = heights >= fraction
    local = 2.0 * np.where(on_right, heights - fraction, heights - fraction + 1.0) - 1.0
    table = np.array(
        [
            [
                np.prod([(at - points[q]) / (points[n] - points[q]) for q in range(N) if q != n])
                for n in range(N)
            ]
            for at in local
        ]
    )
    return table, ~on_right


D = derivative_table()
EVEN = [[float(0.5 * (D[p, q] + D[p, 6 - q])) for q in range(3)] for p in range(3)]
ODD = [[float(0.5 * (D[p, q] - D[p, 6 - q])) for q in range(3)] for p in range(3)]
TO_MID = [float(D[3, q]) for q in range(3)]
FROM_MID = [float(D[p, 3]) for p in range(3)]
TABLES = [mortar_table(substep) for substep in range(SUBSTEPS)]


def dot(weights, values):
    total = weights[0] * values[0]
    for weight, value in zip(weights[1:], values[1:]):
        total = total + weight * value
    return total


def differentiate(v):
    s = [v[i] + v[6 - i] for i in range(3)]
    d = [v[i] - v[6 - i] for i in range(3)]
    odd = [dot(EVEN[p] + [FROM_MID[p]], s + [v[3]]) for p in range(3)]
    even = [dot(ODD[p], d) for p in range(3)]
    mid = dot(TO_MID, d)
    return (
        [even[p] + odd[p] for p in range(3)] + [mid] + [even[p] - odd[p] for p in (2, 1, 0)]
    )


def differentiate_transposed(w):
    s = [w[i] + w[6 - i] for i in range(3)]
    d = [w[i] - w[6 - i] for i in range(3)]
    odd = [dot([ODD[p][q] for p in range(3)] + [TO_MID[q]], s + [w[3]]) for q in range(3)]
    even = [dot([EVEN[p][q] for p in range(3)], d) for q in range(3)]
    mid = dot(FROM_MID, d)
    return (
        [even[q] + odd[q] for q in range(3)] + [mid] + [even[q] - odd[q] for q in (2, 1, 0)]
    )


def along(coeffs, values):
    grad = differentiate(values)
    return differentiate_transposed([c * g for c, g in zip(coeffs, grad)])


def sparse_dot(weights, values):
    terms = [v if w == 1.0 else w * v for w, v in zip(weights, values) if w != 0.0]
    total = terms[0]
    for term in terms[1:]:
        total = total + term
    return total


def lanes():
    return lax.broadcasted_iota(jnp.int32, (8, 128), 1)


def rows():
    return lax.broadcasted_iota(jnp.int32, (8, 128), 0)


class Place(NamedTuple):
    side: jax.Array
    even: jax.Array
    sector: jax.Array
    within: jax.Array
    substep: jax.Array


def place_at(rotation, step):
    whole = lax.div(rotation[step], SUBSTEPS)
    return Place(
        side=lax.axis_index("side"),
        even=lax.rem(lax.axis_index("circ"), 2) == 0,
        sector=lax.div(whole, 128),
        within=lax.rem(whole, 128),
        substep=rotation[step] - SUBSTEPS * whole,
    )


def branch_of(place):
    return place.sector + jnp.where(place.within < 64, 0, CIRC)


def upper_of(side):
    return jnp.where(side % 2 == 0, 6, 0)


def for_each_substep(condition, substep, run):
    for value in range(SUBSTEPS):

        @pl.when(condition & (substep == value))
        def _(value=value):
            table, left = TABLES[value]
            run(table, [int(is_left) for is_left in left])


def copy_and_correct_edges(place, scale, edges, u_in, u):
    lane = lanes()
    first, second = [edge[...] for edge in edges]
    high = jnp.where(place.even, first, second)
    low = jnp.where(place.even, second, first)
    for a in range(N):
        for r in range(N):
            at = a * N + r
            from_low = jnp.where(lane == 0, pltpu.roll(low, (128 - at) % 128, 1), 0.0)
            from_high = jnp.where(lane == 127, pltpu.roll(high, 127 - at, 1), 0.0)
            for c in range(1, 6):
                u[a, r, c] = u_in[a, r, c]
            u[a, r, 0] = u_in[a, r, 0] - scale[a, r, 0] * from_low
            u[a, r, 6] = u_in[a, r, 6] - scale[a, r, 6] * from_high


def left_count(substep):
    counts = [int(left.sum()) for _, left in TABLES]
    return jnp.where(substep == 0, counts[0], jnp.where(substep == 1, counts[1], counts[2]))


def correct_faces(where, scale, pair, big, small, u):
    side, within, substep = where.side, where.within, where.substep
    upper = upper_of(side)
    lane = lanes()
    for r in range(N):
        for c in range(N):
            u[upper, r, c] = u[upper, r, c] - scale[upper, r, c] * pair[r, c]

    @pl.when((side == 1) | (side == 2))
    def _():
        low = (within < 64) == (side == 2)
        place = jnp.where(low, lane, 127 - lane)
        turns = [jnp.where(low, 0, 64), jnp.where(low, 64, 0)]
        lefts = left_count(substep)
        limits = []
        for m in range(N):
            moved = within + jnp.where(m < lefts, 1, 0)
            first = jnp.where(side == 2, moved, 128 - moved)
            limits.append(jnp.where(low, first, 128 - first))
        for at in range(N * N):
            half = pltpu.roll(small[at // 2], turns[at % 2], 1)
            big[at] = jnp.where(place < limits[at % N], half, big[at])

    @pl.when(side == 2)
    def _():
        for r in range(N):
            for m in range(N):
                u[0, r, m] = u[0, r, m] - scale[0, r, m] * big[r * N + m]

    def to_rotor(table, _):
        def add(r, _):
            parts = [big[r * N + m] for m in range(N)]
            for n in range(N):
                part = sparse_dot([float(table[m, n]) for m in range(N)], parts)
                u[6, r, n] = u[6, r, n] - scale[6, r, n] * part
            return 0

        lax.fori_loop(0, N, add, 0)

    for_each_substep(side == 1, substep, to_rotor)


def apply_planes(u, coeffs, reaction, acc, plane_ready):
    def plane(i, _):
        a = lax.rem(i + 1, N)
        plane_ready(i, a)
        for r in range(N):
            values = [u[a, r, c] for c in range(N)]
            out = along([coeffs[2, a, r, c] for c in range(N)], values)
            for c in range(N):
                acc[a, r, c] = out[c] + reaction[a, r, c] * values[c]
        for c in range(N):
            out = along(
                [coeffs[1, a, r, c] for r in range(N)], [u[a, r, c] for r in range(N)]
            )
            for r in range(N):
                acc[a, r, c] = acc[a, r, c] + out[r]
        return 0

    lax.fori_loop(0, N, plane, 0)


def finish(where, u, coeffs, scale, acc, u_out, edge_first, edge_second, column_ready):
    lane = lanes()
    row = rows()

    def column(r, carry):
        high, low = carry
        column_ready(r)
        for c in range(N):
            values = [u[a, r, c] for a in range(N)]
            out = along([coeffs[0, a, r, c] for a in range(N)], values)
            for a in range(N):
                total = acc[a, r, c] + out[a]
                acc[a, r, c] = total
                if 0 < c < 6:
                    u_out[a, r, c] = values[a] - scale[a, r, c] * total
        for a in range(N):
            inner = acc[a, r, 0]
            outer = acc[a, r, 6]
            first = inner + jnp.where(lane == 0, 0.0, pltpu.roll(outer, 1, 1))
            last = outer + jnp.where(lane == 127, 0.0, pltpu.roll(inner, 127, 1))
            u_out[a, r, 0] = u[a, r, 0] - scale[a, r, 0] * first
            u_out[a, r, 6] = u[a, r, 6] - scale[a, r, 6] * last
            at = a * N + r
            high = jnp.where(lane == at, pltpu.roll(outer, at + 1, 1), high)
            low = jnp.where(lane == at, pltpu.roll(inner, at, 1), low)
        return high, low

    zero = jnp.zeros((8, 128), jnp.float32)
    high, low = lax.fori_loop(0, N, column, (zero, zero))
    edge_first[...] = jnp.where(where.even, high, low)
    edge_second[...] = jnp.where(where.even, low, high)
    for a in range(N):
        for c in range(N):
            below = jnp.where(row == 0, 0.0, pltpu.roll(acc[a, 6, c], 1, 0))
            above = jnp.where(row == 7, 0.0, pltpu.roll(acc[a, 0, c], 7, 0))
            u_out[a, 0, c] = u_out[a, 0, c] - scale[a, 0, c] * below
            u_out[a, 6, c] = u_out[a, 6, c] - scale[a, 6, c] * above


def send_faces(where, acc, pair, big, small, face):
    side, within, substep = where.side, where.within, where.substep
    upper = upper_of(side)
    lane = lanes()
    for r in range(N):
        for c in range(N):
            pair[r, c] = acc[upper, r, c]

    def from_rotor(table, _):
        def row(r, _):
            values = [acc[6, r, n] for n in range(N)]
            for m in range(N):
                face[r * N + m] = sparse_dot([float(x) for x in table[m]], values)
            return 0

        lax.fori_loop(0, N, row, 0)

    for_each_substep(side == 1, substep, from_rotor)

    @pl.when(side == 2)
    def _():
        for r in range(N):
            for m in range(N):
                face[r * N + m] = acc[0, r, m]

    @pl.when((side == 1) | (side == 2))
    def _():
        lefts = left_count(substep)
        shifts = []
        for m in range(N):
            moved = within + jnp.where(m < lefts, 1, 0)
            shifts.append(jnp.where(side == 1, moved, 128 - moved))
        half = jnp.where((within < 64) == (side == 1), 0, 64)
        for at in range(N * N):
            big[at] = pltpu.roll(face[at], lax.rem(shifts[at % N], 128), 1)
        for g in range((N * N + 1) // 2):
            first = pltpu.roll(face[2 * g], lax.rem(shifts[2 * g % N] + half, 128), 1)
            at = min(2 * g + 1, N * N - 1)
            second = pltpu.roll(face[at], lax.rem(shifts[at % N] + 64 + half, 128), 1)
            small[g] = jnp.where(lane < 64, first, second)


def loads(coeffs, reaction, coeffs_v, reaction_v, sems):
    def plane_copies(a):
        return [
            pltpu.make_async_copy(coeffs.at[2, a], coeffs_v.at[2, a], sems.at[a]),
            pltpu.make_async_copy(coeffs.at[1, a], coeffs_v.at[1, a], sems.at[7 + a]),
            pltpu.make_async_copy(reaction.at[a], reaction_v.at[a], sems.at[14 + a]),
        ]

    def column_copy(r):
        return pltpu.make_async_copy(
            coeffs.at[0, :, r], coeffs_v.at[0, :, r], sems.at[21 + r]
        )

    return plane_copies, column_copy


def first_kernel(
    rotation, field, coeffs, reaction, scale,
    u_out, pair, big, small, edge_first, edge_second, scale_v, branch,
    acc, coeffs_v, reaction_v, u, face, sems,
):
    where = place_at(rotation, 0)
    branch[...] = jnp.full((8, 128), branch_of(where), jnp.int32)
    plane_copies, column_copy = loads(coeffs, reaction, coeffs_v, reaction_v, sems)
    field_copies = [pltpu.make_async_copy(field.at[a], u.at[a], sems.at[30 + a]) for a in range(N)]
    scale_copy = pltpu.make_async_copy(scale, scale_v, sems.at[28])
    for i in range(N):
        a = (i + 1) % N
        field_copies[a].start()
        for copy in plane_copies(a):
            copy.start()
    scale_copy.start()
    for r in range(N):
        column_copy(r).start()

    def plane_ready(i, a):
        pltpu.make_async_copy(field.at[a], u.at[a], sems.at[30 + a]).wait()
        for copy in plane_copies(a):
            copy.wait()

    apply_planes(u, coeffs_v, reaction_v, acc, plane_ready)
    scale_copy.wait()
    finish(
        where, u, coeffs_v, scale_v, acc, u_out, edge_first, edge_second,
        lambda r: column_copy(r).wait(),
    )
    send_faces(where, acc, pair, big, small, face)


def step_kernel(
    rotation, at_step, u_in, scale, coeffs, reaction, pair_in, big_in, small_in,
    first_in, second_in,
    u_out, pair, big, small, edge_first, edge_second, _scale, branch,
    acc, coeffs_v, reaction_v, u, big_v, small_v, sems,
):
    step = at_step[0]
    more = step < STEPS - 1
    was = place_at(rotation, step)
    where = place_at(rotation, jnp.minimum(step + 1, STEPS - 1))
    branch[...] = jnp.full((8, 128), branch_of(where), jnp.int32)
    plane_copies, column_copy = loads(coeffs, reaction, coeffs_v, reaction_v, sems)
    big_copy = pltpu.make_async_copy(big_in, big_v, sems.at[28])
    small_copy = pltpu.make_async_copy(small_in, small_v, sems.at[29])
    edges = (first_in, second_in)

    @pl.when(more)
    def _():
        for i in range(N):
            for copy in plane_copies((i + 1) % N):
                copy.start()
            if i == 2:
                big_copy.start()
                small_copy.start()
        for r in range(N):
            column_copy(r).start()

    def faces():
        big_copy.wait()
        small_copy.wait()
        correct_faces(was, scale, pair_in, big_v, small_v, u)

    copy_and_correct_edges(was, scale, edges, u_in, u)

    @pl.when(more)
    def _():
        def plane_ready(i, a):
            for copy in plane_copies(a):
                copy.wait()

            @pl.when(i == N - 2)
            def _():
                faces()

        apply_planes(u, coeffs_v, reaction_v, acc, plane_ready)
        finish(
            where, u, coeffs_v, scale, acc, u_out, edge_first, edge_second,
            lambda r: column_copy(r).wait(),
        )
        send_faces(where, acc, pair, big, small, big_v)

    @pl.when(step == STEPS - 1)
    def _():
        big_copy.start()
        small_copy.start()
        faces()

        def copy(a, _):
            for r in range(N):
                for c in range(N):
                    u_out[a, r, c] = u[a, r, c]
            return 0

        lax.fori_loop(0, N, copy, 0)


def at(circ, side):
    return (circ % CIRC) * SIDES + side


EVERY = [(c, s) for c in range(CIRC) for s in range(SIDES)]
PAIR = [(at(c, s), at(c, s ^ 1)) for c, s in EVERY]
SWAP_FIRST = [(at(c, s), at(c ^ 1, s)) for c, s in EVERY]
SWAP_SECOND = [(at(c, s), at(c + (1 if c % 2 else -1), s)) for c, s in EVERY]


def rotated(hops):
    pairs = []
    for c in range(CIRC):
        pairs.append((at(c, 1), at(c + hops, 2)))
        pairs.append((at(c, 2), at(c - hops, 1)))
    return pairs


def exchange(big_hops, small_hops, big, small):
    big = lax.ppermute(big, AXES, rotated(big_hops))
    return big, lax.ppermute(small, AXES, rotated(small_hops))


def local(field, coeffs, reaction, step_scale, rotation):
    field, coeffs, reaction, step_scale = field[0], coeffs[0], reaction[0], step_scale[0]
    branches = [lambda *v, h=h: exchange(h, h + 1, *v) for h in range(CIRC)]
    branches += [lambda *v, h=h: exchange(h + 1, h, *v) for h in range(CIRC)]

    array = lambda *shape: jax.ShapeDtypeStruct(shape, jnp.float32)
    node = pltpu.VMEM(field.shape, jnp.float32)
    face, edge = array(*field.shape[1:]), array(8, 128)
    sends = (node, face, array(49, 8, 128), array(25, 8, 128), edge, edge, node)
    sends += (jax.ShapeDtypeStruct((8, 128), jnp.int32),)
    vmem = pl.BlockSpec(memory_space=pltpu.VMEM)
    smem = pl.BlockSpec(memory_space=pltpu.SMEM)
    hbm = pl.BlockSpec(memory_space=pltpu.HBM)
    buffers = [pltpu.VMEM(shape, jnp.float32) for shape in (field.shape, coeffs.shape, field.shape)]
    bigger = pltpu.VMEM((49, 8, 128), jnp.float32)
    params = pltpu.CompilerParams(vmem_limit_bytes=VMEM_LIMIT)
    field, coeffs, reaction, step_scale = [
        pltpu.with_memory_space_constraint(x, pltpu.HBM)
        for x in (field, coeffs, reaction, step_scale)
    ]
    carry = pl.pallas_call(
        first_kernel,
        out_shape=sends,
        in_specs=[smem] + [hbm] * 4,
        out_specs=(vmem,) * 8,
        scratch_shapes=buffers + [buffers[0], bigger, pltpu.SemaphoreType.DMA((37,))],
        compiler_params=params,
        name="first",
    )(rotation, field, coeffs, reaction, step_scale)
    advance = pl.pallas_call(
        step_kernel,
        out_shape=sends,
        in_specs=[smem, smem, vmem, vmem, hbm, hbm, vmem, hbm, hbm, vmem, vmem],
        out_specs=(vmem,) * 8,
        scratch_shapes=buffers
        + [buffers[0], bigger, pltpu.VMEM((25, 8, 128), jnp.float32)]
        + [pltpu.SemaphoreType.DMA((30,))],
        input_output_aliases={2: 0, 3: 6},
        compiler_params=params,
        name="step",
    )

    def body(step, carry):
        u, pair, big, small, first, second, scale, branch = carry
        pair = lax.ppermute(pair, AXES, PAIR)
        first = lax.ppermute(first, AXES, SWAP_FIRST)
        second = lax.ppermute(second, AXES, SWAP_SECOND)
        big, small = lax.switch(branch[0, 0], branches, big, small)
        streamed = [pltpu.with_memory_space_constraint(x, pltpu.HBM) for x in (coeffs, reaction)]
        return advance(
            rotation, step[None], u, scale, *streamed, pair, big, small, first, second
        )

    return lax.fori_loop(0, STEPS, body, tuple(carry))[0][None]


def solution(mesh):
    in_specs = (
        P("side", None, None, None, None, "circ"),
        P("side", None, None, None, None, None, "circ"),
        P("side", None, None, None, None, "circ"),
        P("side", None, None, None, None, "circ"),
        P(),
    )
    out_specs = P("side", None, None, None, None, "circ")
    return jax.shard_map(local, mesh=mesh, in_specs=in_specs, out_specs=out_specs, check_vma=False)
```

profile of v0, /device:TPU:1, one launch (start us, length us, event | category | flops | bytes accessed | tf_op | source)
XLA Modules:
  0.0 107.8 jit_solution(257996317683015988)
XLA Ops:
  0.0 5.7 %first.1 = (f32[7,7,7,8,128]{4,3,2,1,0:T(8,128)S(1)}, f32[7,7,8,128]{3,2,1,0:T(8,128)S(1)}, f32[49,8,128]{2,1,0:T(8,128)S(1)}, f32[25,8,128]{2,1,0:T(8,128)S(1)}...) custom-call(s32[4]{0:T(128)} %rotation.1, ...), custom_call_target="tpu_custom_call" | custom-call | tf_op jit(solution)/shard_map/first/pallas_call | solution.py:482
  5.8 100.9 %while.27 = (s32[]{:T(128)}, f32[7,7,7,8,128]{4,3,2,1,0:T(8,128)S(1)}, f32[7,7,8,128]{3,2,1,0:T(8,128)S(1)}, f32[49,8,128]{2,1,0:T(8,128)S(1)}, f32[25,8,128]{2,...) while((s32[]{:T(128)}, ...), condition=%wide.region_65.0_spmd, body=%wide.region_0.0_spmd.sunk | while | flops 3 | bytes 2048405 | solution.py:515
  6.9 8.8 %collective-permute-start.130 = (f32[8,128]{1,0:T(8,128)S(1)}, f32[8,128]{1,0:T(8,128)S(1)}, u32[]{:S(2)}, u32[]{:S(2)}) collective-permute-start(f32[8,128]{1,0:T(8,128)S(1)} %get-tuple-element.885), channel_id=1, source_target_pairs={{0,124},{1,125},{2,126},{3,127},{4,8},{5,9},{6,10},{7,11},{8,4},{9... | collective-permute-start | bytes 12296 | tf_op jit(solution)/shard_map/while/body/eval_jaxpr/ppermute | solution.py:508
  16.8 12.0 %conditional.2 = (f32[49,8,128]{2,1,0:T(8,128)}, f32[25,8,128]{2,1,0:T(8,128)}) conditional(s32[]{:T(128)} %bitcast.10, (f32[49,8,128]{2,1,0:T(8,128)S(1)}, f32[25,8,128]{2,1,0:T(8,128)S(1)}) %tuple.285, (f32[49,8,128]{2,1,0:T(8,128)S(1)}, f32[25,8,128]{2,1,0:T(8,128)S(1)}) %tuple.285, (f32[49,8,128]{2,1,0:T(8,128)S(1)}, ...), branch_computations={%region_1.0_spmd, %region_2.0_spmd, %region_3.0_spmd, %region_4.0_... | conditional | bytes 1212512 | solution.py:509
  16.8 2.3 %collective-permute-start.82 = (f32[49,8,128]{2,1,0:T(8,128)S(1)}, f32[49,8,128]{2,1,0:T(8,128)}, u32[]{:S(2)}, u32[]{:S(2)}) collective-permute-start(f32[49,8,128]{2,1,0:T(8,128)S(1)} %get-tuple-element.532), channel_id=1, source_target_pairs={{1,42},{2,89},{5,46},{6,93},{9,50},{10,97},{13,54},{14,101},{17,58... | collective-permute-start | bytes 602120 | tf_op jit(solution)/shard_map/while/body/eval_jaxpr/cond/branch_41_fun/ppermute | solution.py:458
  19.1 2.8 %collective-permute-start.83 = (f32[25,8,128]{2,1,0:T(8,128)S(1)}, f32[25,8,128]{2,1,0:T(8,128)}, u32[]{:S(2)}, u32[]{:S(2)}) collective-permute-start(f32[25,8,128]{2,1,0:T(8,128)S(1)} %get-tuple-element.533), channel_id=1, source_target_pairs={{1,38},{2,93},{5,42},{6,97},{9,46},{10,101},{13,50},{14,105},{17,5... | collective-permute-start | bytes 307208 | tf_op jit(solution)/shard_map/while/body/eval_jaxpr/cond/branch_41_fun/ppermute | solution.py:459
  21.9 6.6 %collective-permute-done.83 = f32[25,8,128]{2,1,0:T(8,128)} collective-permute-done((f32[25,8,128]{2,1,0:T(8,128)S(1)}, f32[25,8,128]{2,1,0:T(8,128)}, u32[]{:S(2)}, u32[]{:S(2)}) %collective-permute-start.83) | collective-permute-done | bytes 102432 | tf_op jit(solution)/shard_map/while/body/eval_jaxpr/cond/branch_41_fun/ppermute | solution.py:459
  28.8 5.6 %step.5 = (f32[7,7,7,8,128]{4,3,2,1,0:T(8,128)S(1)}, f32[7,7,8,128]{3,2,1,0:T(8,128)S(1)}, f32[49,8,128]{2,1,0:T(8,128)S(1)}, f32[25,8,128]{2,1,0:T(8,128)S(1)},...) custom-call(s32[4]{0:T(128)S(1)} %get-tuple-element.903.rotation, ...), custom_call_target="tpu_custom_call", output_to_operand_aliasing={{0}: (2, {}), {6}: (3, {})} | custom-call | tf_op jit(solution)/shard_map/while/body/eval_jaxpr/step/pallas_call | solution.py:511
  34.5 3.8 %collective-permute-start.130 = (f32[8,128]{1,0:T(8,128)S(1)}, f32[8,128]{1,0:T(8,128)S(1)}, u32[]{:S(2)}, u32[]{:S(2)}) collective-permute-start(f32[8,128]{1,0:T(8,128)S(1)} %get-tuple-element.885), channel_id=1, source_target_pairs={{0,124},{1,125},{2,126},{3,127},{4,8},{5,9},{6,10},{7,11},{8,4},{9... | collective-permute-start | bytes 12296 | tf_op jit(solution)/shard_map/while/body/eval_jaxpr/ppermute | solution.py:508
  39.4 18.2 %conditional.2 = (f32[49,8,128]{2,1,0:T(8,128)}, f32[25,8,128]{2,1,0:T(8,128)}) conditional(s32[]{:T(128)} %bitcast.10, (f32[49,8,128]{2,1,0:T(8,128)S(1)}, f32[25,8,128]{2,1,0:T(8,128)S(1)}) %tuple.285, (f32[49,8,128]{2,1,0:T(8,128)S(1)}, f32[25,8,128]{2,1,0:T(8,128)S(1)}) %tuple.285, (f32[49,8,128]{2,1,0:T(8,128)S(1)}, ...), branch_computations={%region_1.0_spmd, %region_2.0_spmd, %region_3.0_spmd, %region_4.0_... | conditional | bytes 1212512 | solution.py:509
  39.4 7.8 %collective-permute-start.28 = (f32[49,8,128]{2,1,0:T(8,128)S(1)}, f32[49,8,128]{2,1,0:T(8,128)}, u32[]{:S(2)}, u32[]{:S(2)}) collective-permute-start(f32[49,8,128]{2,1,0:T(8,128)S(1)} %get-tuple-element.478), channel_id=1, source_target_pairs={{1,58},{2,73},{5,62},{6,77},{9,66},{10,81},{13,70},{14,85},{17,74}... | collective-permute-start | bytes 602120 | tf_op jit(solution)/shard_map/while/body/eval_jaxpr/cond/branch_14_fun/ppermute | solution.py:458
  47.2 3.2 %collective-permute-start.29 = (f32[25,8,128]{2,1,0:T(8,128)S(1)}, f32[25,8,128]{2,1,0:T(8,128)}, u32[]{:S(2)}, u32[]{:S(2)}) collective-permute-start(f32[25,8,128]{2,1,0:T(8,128)S(1)} %get-tuple-element.479), channel_id=1, source_target_pairs={{1,62},{2,69},{5,66},{6,73},{9,70},{10,77},{13,74},{14,81},{17,78}... | collective-permute-start | bytes 307208 | tf_op jit(solution)/shard_map/while/body/eval_jaxpr/cond/branch_14_fun/ppermute | solution.py:459
  50.4 7.1 %collective-permute-done.29 = f32[25,8,128]{2,1,0:T(8,128)} collective-permute-done((f32[25,8,128]{2,1,0:T(8,128)S(1)}, f32[25,8,128]{2,1,0:T(8,128)}, u32[]{:S(2)}, u32[]{:S(2)}) %collective-permute-start.29) | collective-permute-done | bytes 102432 | tf_op jit(solution)/shard_map/while/body/eval_jaxpr/cond/branch_14_fun/ppermute | solution.py:459
  57.6 5.6 %step.5 = (f32[7,7,7,8,128]{4,3,2,1,0:T(8,128)S(1)}, f32[7,7,8,128]{3,2,1,0:T(8,128)S(1)}, f32[49,8,128]{2,1,0:T(8,128)S(1)}, f32[25,8,128]{2,1,0:T(8,128)S(1)},...) custom-call(s32[4]{0:T(128)S(1)} %get-tuple-element.903.rotation, ...), custom_call_target="tpu_custom_call", output_to_operand_aliasing={{0}: (2, {}), {6}: (3, {})} | custom-call | tf_op jit(solution)/shard_map/while/body/eval_jaxpr/step/pallas_call | solution.py:511
  64.5 13.2 %conditional.2 = (f32[49,8,128]{2,1,0:T(8,128)}, f32[25,8,128]{2,1,0:T(8,128)}) conditional(s32[]{:T(128)} %bitcast.10, (f32[49,8,128]{2,1,0:T(8,128)S(1)}, f32[25,8,128]{2,1,0:T(8,128)S(1)}) %tuple.285, (f32[49,8,128]{2,1,0:T(8,128)S(1)}, f32[25,8,128]{2,1,0:T(8,128)S(1)}) %tuple.285, (f32[49,8,128]{2,1,0:T(8,128)S(1)}, ...), branch_computations={%region_1.0_spmd, %region_2.0_spmd, %region_3.0_spmd, %region_4.0_... | conditional | bytes 1212512 | solution.py:509
  64.5 6.2 %collective-permute-start = (f32[49,8,128]{2,1,0:T(8,128)S(1)}, f32[49,8,128]{2,1,0:T(8,128)}, u32[]{:S(2)}, u32[]{:S(2)}) collective-permute-start(f32[49,8,128]{2,1,0:T(8,128)S(1)} %get-tuple-element.450), channel_id=1, source_target_pairs={{1,2},{2,1},{5,6},{6,5},{9,10},{10,9},{13,14},{14,13},{17,18},{18,... | collective-permute-start | bytes 602120 | tf_op jit(solution)/shard_map/while/body/eval_jaxpr/cond/branch_0_fun/ppermute | solution.py:458
  70.8 3.4 %collective-permute-start.1 = (f32[25,8,128]{2,1,0:T(8,128)S(1)}, f32[25,8,128]{2,1,0:T(8,128)}, u32[]{:S(2)}, u32[]{:S(2)}) collective-permute-start(f32[25,8,128]{2,1,0:T(8,128)S(1)} %get-tuple-element.451), channel_id=1, source_target_pairs={{1,6},{2,125},{5,10},{6,1},{9,14},{10,5},{13,18},{14,9},{17,22},{1... | collective-permute-start | bytes 307208 | tf_op jit(solution)/shard_map/while/body/eval_jaxpr/cond/branch_0_fun/ppermute | solution.py:459
  74.1 3.6 %collective-permute-done.1 = f32[25,8,128]{2,1,0:T(8,128)} collective-permute-done((f32[25,8,128]{2,1,0:T(8,128)S(1)}, f32[25,8,128]{2,1,0:T(8,128)}, u32[]{:S(2)}, u32[]{:S(2)}) %collective-permute-start.1) | collective-permute-done | bytes 102432 | tf_op jit(solution)/shard_map/while/body/eval_jaxpr/cond/branch_0_fun/ppermute | solution.py:459
  77.8 5.5 %step.5 = (f32[7,7,7,8,128]{4,3,2,1,0:T(8,128)S(1)}, f32[7,7,8,128]{3,2,1,0:T(8,128)S(1)}, f32[49,8,128]{2,1,0:T(8,128)S(1)}, f32[25,8,128]{2,1,0:T(8,128)S(1)},...) custom-call(s32[4]{0:T(128)S(1)} %get-tuple-element.903.rotation, ...), custom_call_target="tpu_custom_call", output_to_operand_aliasing={{0}: (2, {}), {6}: (3, {})} | custom-call | tf_op jit(solution)/shard_map/while/body/eval_jaxpr/step/pallas_call | solution.py:511
  83.4 6.2 %collective-permute-start.130 = (f32[8,128]{1,0:T(8,128)S(1)}, f32[8,128]{1,0:T(8,128)S(1)}, u32[]{:S(2)}, u32[]{:S(2)}) collective-permute-start(f32[8,128]{1,0:T(8,128)S(1)} %get-tuple-element.885), channel_id=1, source_target_pairs={{0,124},{1,125},{2,126},{3,127},{4,8},{5,9},{6,10},{7,11},{8,4},{9... | collective-permute-start | bytes 12296 | tf_op jit(solution)/shard_map/while/body/eval_jaxpr/ppermute | solution.py:508
  90.7 13.5 %conditional.2 = (f32[49,8,128]{2,1,0:T(8,128)}, f32[25,8,128]{2,1,0:T(8,128)}) conditional(s32[]{:T(128)} %bitcast.10, (f32[49,8,128]{2,1,0:T(8,128)S(1)}, f32[25,8,128]{2,1,0:T(8,128)S(1)}) %tuple.285, (f32[49,8,128]{2,1,0:T(8,128)S(1)}, f32[25,8,128]{2,1,0:T(8,128)S(1)}) %tuple.285, (f32[49,8,128]{2,1,0:T(8,128)S(1)}, ...), branch_computations={%region_1.0_spmd, %region_2.0_spmd, %region_3.0_spmd, %region_4.0_... | conditional | bytes 1212512 | solution.py:509
  92.7 5.9 %collective-permute-start.127 = (f32[25,8,128]{2,1,0:T(8,128)S(1)}, f32[25,8,128]{2,1,0:T(8,128)}, u32[]{:S(2)}, u32[]{:S(2)}) collective-permute-start(f32[25,8,128]{2,1,0:T(8,128)S(1)} %get-tuple-element.577), channel_id=1, source_target_pairs={{1,126},{2,5},{5,2},{6,9},{9,6},{10,13},{13,10},{14,17},{17,14},{1... | collective-permute-start | bytes 307208 | tf_op jit(solution)/shard_map/while/body/eval_jaxpr/cond/branch_63_fun/ppermute | solution.py:459
  98.6 5.6 %collective-permute-done.127 = f32[25,8,128]{2,1,0:T(8,128)} collective-permute-done((f32[25,8,128]{2,1,0:T(8,128)S(1)}, f32[25,8,128]{2,1,0:T(8,128)}, u32[]{:S(2)}, u32[]{:S(2)}) %collective-permute-start.127) | collective-permute-done | bytes 102432 | tf_op jit(solution)/shard_map/while/body/eval_jaxpr/cond/branch_63_fun/ppermute | solution.py:459
  104.2 2.5 %step.5 = (f32[7,7,7,8,128]{4,3,2,1,0:T(8,128)S(1)}, f32[7,7,8,128]{3,2,1,0:T(8,128)S(1)}, f32[49,8,128]{2,1,0:T(8,128)S(1)}, f32[25,8,128]{2,1,0:T(8,128)S(1)},...) custom-call(s32[4]{0:T(128)S(1)} %get-tuple-element.903.rotation, ...), custom_call_target="tpu_custom_call", output_to_operand_aliasing={{0}: (2, {}), {6}: (3, {})} | custom-call | tf_op jit(solution)/shard_map/while/body/eval_jaxpr/step/pallas_call | solution.py:511
  (33 shorter events, 6.9 us)
Async XLA Ops:
  0.0 5.8 %copy-start = (s32[4]{0:T(128)S(1)}, s32[4]{0:T(128)}, u32[]{:S(2)}) copy-start(s32[4]{0:T(128)} %rotation.1) | copy-start | bytes 52
  5.8 23.0 %collective-permute-start.128 = (f32[7,7,8,128]{3,2,1,0:T(8,128)S(1)}, f32[7,7,8,128]{3,2,1,0:T(8,128)S(1)}, u32[]{:S(2)}, u32[]{:S(2)}) collective-permute-start(f32[7,7,8,128]{3,2,1,0:T(8,128)S(1)} %get-tuple-element.881), channel_id=1, source_target_pairs={{0,1},{1,0},{2,3},{3,2},{4,5},{5,4},{6,7},{7,6},{8,9},{9,8},{10,11... | collective-permute-start | bytes 602120 | tf_op jit(solution)/shard_map/while/body/eval_jaxpr/ppermute | solution.py:506
  6.9 21.8 %collective-permute-start.130 = (f32[8,128]{1,0:T(8,128)S(1)}, f32[8,128]{1,0:T(8,128)S(1)}, u32[]{:S(2)}, u32[]{:S(2)}) collective-permute-start(f32[8,128]{1,0:T(8,128)S(1)} %get-tuple-element.885), channel_id=1, source_target_pairs={{0,124},{1,125},{2,126},{3,127},{4,8},{5,9},{6,10},{7,11},{8,4},{9... | collective-permute-start | bytes 12296 | tf_op jit(solution)/shard_map/while/body/eval_jaxpr/ppermute | solution.py:508
  15.7 13.1 %collective-permute-start.129 = (f32[8,128]{1,0:T(8,128)S(1)}, f32[8,128]{1,0:T(8,128)S(1)}, u32[]{:S(2)}, u32[]{:S(2)}) collective-permute-start(f32[8,128]{1,0:T(8,128)S(1)} %get-tuple-element.884), channel_id=1, source_target_pairs={{0,4},{1,5},{2,6},{3,7},{4,0},{5,1},{6,2},{7,3},{8,12},{9,13},{10,... | collective-permute-start | bytes 12296 | tf_op jit(solution)/shard_map/while/body/eval_jaxpr/ppermute | solution.py:507
  16.8 11.9 %collective-permute-start.82 = (f32[49,8,128]{2,1,0:T(8,128)S(1)}, f32[49,8,128]{2,1,0:T(8,128)}, u32[]{:S(2)}, u32[]{:S(2)}) collective-permute-start(f32[49,8,128]{2,1,0:T(8,128)S(1)} %get-tuple-element.532), channel_id=1, source_target_pairs={{1,42},{2,89},{5,46},{6,93},{9,50},{10,97},{13,54},{14,101},{17,58... | collective-permute-start | bytes 602120 | tf_op jit(solution)/shard_map/while/body/eval_jaxpr/cond/branch_41_fun/ppermute | solution.py:458
  19.1 9.4 %collective-permute-start.83 = (f32[25,8,128]{2,1,0:T(8,128)S(1)}, f32[25,8,128]{2,1,0:T(8,128)}, u32[]{:S(2)}, u32[]{:S(2)}) collective-permute-start(f32[25,8,128]{2,1,0:T(8,128)S(1)} %get-tuple-element.533), channel_id=1, source_target_pairs={{1,38},{2,93},{5,42},{6,97},{9,46},{10,101},{13,50},{14,105},{17,5... | collective-permute-start | bytes 307208 | tf_op jit(solution)/shard_map/while/body/eval_jaxpr/cond/branch_41_fun/ppermute | solution.py:459
  34.4 23.1 %collective-permute-start.128 = (f32[7,7,8,128]{3,2,1,0:T(8,128)S(1)}, f32[7,7,8,128]{3,2,1,0:T(8,128)S(1)}, u32[]{:S(2)}, u32[]{:S(2)}) collective-permute-start(f32[7,7,8,128]{3,2,1,0:T(8,128)S(1)} %get-tuple-element.881), channel_id=1, source_target_pairs={{0,1},{1,0},{2,3},{3,2},{4,5},{5,4},{6,7},{7,6},{8,9},{9,8},{10,11... | collective-permute-start | bytes 602120 | tf_op jit(solution)/shard_map/while/body/eval_jaxpr/ppermute | solution.py:506
  34.5 23.0 %collective-permute-start.130 = (f32[8,128]{1,0:T(8,128)S(1)}, f32[8,128]{1,0:T(8,128)S(1)}, u32[]{:S(2)}, u32[]{:S(2)}) collective-permute-start(f32[8,128]{1,0:T(8,128)S(1)} %get-tuple-element.885), channel_id=1, source_target_pairs={{0,124},{1,125},{2,126},{3,127},{4,8},{5,9},{6,10},{7,11},{8,4},{9... | collective-permute-start | bytes 12296 | tf_op jit(solution)/shard_map/while/body/eval_jaxpr/ppermute | solution.py:508
  38.3 19.2 %collective-permute-start.129 = (f32[8,128]{1,0:T(8,128)S(1)}, f32[8,128]{1,0:T(8,128)S(1)}, u32[]{:S(2)}, u32[]{:S(2)}) collective-permute-start(f32[8,128]{1,0:T(8,128)S(1)} %get-tuple-element.884), channel_id=1, source_target_pairs={{0,4},{1,5},{2,6},{3,7},{4,0},{5,1},{6,2},{7,3},{8,12},{9,13},{10,... | collective-permute-start | bytes 12296 | tf_op jit(solution)/shard_map/while/body/eval_jaxpr/ppermute | solution.py:507
  39.4 18.1 %collective-permute-start.28 = (f32[49,8,128]{2,1,0:T(8,128)S(1)}, f32[49,8,128]{2,1,0:T(8,128)}, u32[]{:S(2)}, u32[]{:S(2)}) collective-permute-start(f32[49,8,128]{2,1,0:T(8,128)S(1)} %get-tuple-element.478), channel_id=1, source_target_pairs={{1,58},{2,73},{5,62},{6,77},{9,66},{10,81},{13,70},{14,85},{17,74}... | collective-permute-start | bytes 602120 | tf_op jit(solution)/shard_map/while/body/eval_jaxpr/cond/branch_14_fun/ppermute | solution.py:458
  47.2 10.3 %collective-permute-start.29 = (f32[25,8,128]{2,1,0:T(8,128)S(1)}, f32[25,8,128]{2,1,0:T(8,128)}, u32[]{:S(2)}, u32[]{:S(2)}) collective-permute-start(f32[25,8,128]{2,1,0:T(8,128)S(1)} %get-tuple-element.479), channel_id=1, source_target_pairs={{1,62},{2,69},{5,66},{6,73},{9,70},{10,77},{13,74},{14,81},{17,78}... | collective-permute-start | bytes 307208 | tf_op jit(solution)/shard_map/while/body/eval_jaxpr/cond/branch_14_fun/ppermute | solution.py:459
  63.2 14.6 %collective-permute-start.128 = (f32[7,7,8,128]{3,2,1,0:T(8,128)S(1)}, f32[7,7,8,128]{3,2,1,0:T(8,128)S(1)}, u32[]{:S(2)}, u32[]{:S(2)}) collective-permute-start(f32[7,7,8,128]{3,2,1,0:T(8,128)S(1)} %get-tuple-element.881), channel_id=1, source_target_pairs={{0,1},{1,0},{2,3},{3,2},{4,5},{5,4},{6,7},{7,6},{8,9},{9,8},{10,11... | collective-permute-start | bytes 602120 | tf_op jit(solution)/shard_map/while/body/eval_jaxpr/ppermute | solution.py:506
  63.2 14.5 %collective-permute-start.130 = (f32[8,128]{1,0:T(8,128)S(1)}, f32[8,128]{1,0:T(8,128)S(1)}, u32[]{:S(2)}, u32[]{:S(2)}) collective-permute-start(f32[8,128]{1,0:T(8,128)S(1)} %get-tuple-element.885), channel_id=1, source_target_pairs={{0,124},{1,125},{2,126},{3,127},{4,8},{5,9},{6,10},{7,11},{8,4},{9... | collective-permute-start | bytes 12296 | tf_op jit(solution)/shard_map/while/body/eval_jaxpr/ppermute | solution.py:508
  63.3 14.4 %collective-permute-start.129 = (f32[8,128]{1,0:T(8,128)S(1)}, f32[8,128]{1,0:T(8,128)S(1)}, u32[]{:S(2)}, u32[]{:S(2)}) collective-permute-start(f32[8,128]{1,0:T(8,128)S(1)} %get-tuple-element.884), channel_id=1, source_target_pairs={{0,4},{1,5},{2,6},{3,7},{4,0},{5,1},{6,2},{7,3},{8,12},{9,13},{10,... | collective-permute-start | bytes 12296 | tf_op jit(solution)/shard_map/while/body/eval_jaxpr/ppermute | solution.py:507
  64.5 13.2 %collective-permute-start = (f32[49,8,128]{2,1,0:T(8,128)S(1)}, f32[49,8,128]{2,1,0:T(8,128)}, u32[]{:S(2)}, u32[]{:S(2)}) collective-permute-start(f32[49,8,128]{2,1,0:T(8,128)S(1)} %get-tuple-element.450), channel_id=1, source_target_pairs={{1,2},{2,1},{5,6},{6,5},{9,10},{10,9},{13,14},{14,13},{17,18},{18,... | collective-permute-start | bytes 602120 | tf_op jit(solution)/shard_map/while/body/eval_jaxpr/cond/branch_0_fun/ppermute | solution.py:458
  70.8 7.0 %collective-permute-start.1 = (f32[25,8,128]{2,1,0:T(8,128)S(1)}, f32[25,8,128]{2,1,0:T(8,128)}, u32[]{:S(2)}, u32[]{:S(2)}) collective-permute-start(f32[25,8,128]{2,1,0:T(8,128)S(1)} %get-tuple-element.451), channel_id=1, source_target_pairs={{1,6},{2,125},{5,10},{6,1},{9,14},{10,5},{13,18},{14,9},{17,22},{1... | collective-permute-start | bytes 307208 | tf_op jit(solution)/shard_map/while/body/eval_jaxpr/cond/branch_0_fun/ppermute | solution.py:459
  83.3 20.9 %collective-permute-start.128 = (f32[7,7,8,128]{3,2,1,0:T(8,128)S(1)}, f32[7,7,8,128]{3,2,1,0:T(8,128)S(1)}, u32[]{:S(2)}, u32[]{:S(2)}) collective-permute-start(f32[7,7,8,128]{3,2,1,0:T(8,128)S(1)} %get-tuple-element.881), channel_id=1, source_target_pairs={{0,1},{1,0},{2,3},{3,2},{4,5},{5,4},{6,7},{7,6},{8,9},{9,8},{10,11... | collective-permute-start | bytes 602120 | tf_op jit(solution)/shard_map/while/body/eval_jaxpr/ppermute | solution.py:506
  83.4 20.8 %collective-permute-start.130 = (f32[8,128]{1,0:T(8,128)S(1)}, f32[8,128]{1,0:T(8,128)S(1)}, u32[]{:S(2)}, u32[]{:S(2)}) collective-permute-start(f32[8,128]{1,0:T(8,128)S(1)} %get-tuple-element.885), channel_id=1, source_target_pairs={{0,124},{1,125},{2,126},{3,127},{4,8},{5,9},{6,10},{7,11},{8,4},{9... | collective-permute-start | bytes 12296 | tf_op jit(solution)/shard_map/while/body/eval_jaxpr/ppermute | solution.py:508
  89.6 14.6 %collective-permute-start.129 = (f32[8,128]{1,0:T(8,128)S(1)}, f32[8,128]{1,0:T(8,128)S(1)}, u32[]{:S(2)}, u32[]{:S(2)}) collective-permute-start(f32[8,128]{1,0:T(8,128)S(1)} %get-tuple-element.884), channel_id=1, source_target_pairs={{0,4},{1,5},{2,6},{3,7},{4,0},{5,1},{6,2},{7,3},{8,12},{9,13},{10,... | collective-permute-start | bytes 12296 | tf_op jit(solution)/shard_map/while/body/eval_jaxpr/ppermute | solution.py:507
  90.7 13.4 %collective-permute-start.126 = (f32[49,8,128]{2,1,0:T(8,128)S(1)}, f32[49,8,128]{2,1,0:T(8,128)}, u32[]{:S(2)}, u32[]{:S(2)}) collective-permute-start(f32[49,8,128]{2,1,0:T(8,128)S(1)} %get-tuple-element.576), channel_id=1, source_target_pairs={{1,2},{2,1},{5,6},{6,5},{9,10},{10,9},{13,14},{14,13},{17,18},{18,... | collective-permute-start | bytes 602120 | tf_op jit(solution)/shard_map/while/body/eval_jaxpr/cond/branch_63_fun/ppermute | solution.py:458
  92.7 11.5 %collective-permute-start.127 = (f32[25,8,128]{2,1,0:T(8,128)S(1)}, f32[25,8,128]{2,1,0:T(8,128)}, u32[]{:S(2)}, u32[]{:S(2)}) collective-permute-start(f32[25,8,128]{2,1,0:T(8,128)S(1)} %get-tuple-element.577), channel_id=1, source_target_pairs={{1,126},{2,5},{5,2},{6,9},{9,6},{10,13},{13,10},{14,17},{17,14},{1... | collective-permute-start | bytes 307208 | tf_op jit(solution)/shard_map/while/body/eval_jaxpr/cond/branch_63_fun/ppermute | solution.py:459
where the time goes:
time: 106 us; the launch traced here: 108 us
  starting transfers between devices  53.8 us (51%)
  Pallas kernels  24.9 us (23%)
  waiting for transfers between devices  23.2 us (22%)
  local copies, waits for them, and re-layouts  3.11 us (3%)
  loops' own time  2.67 us (3%)
    ppermute x4, waiting for transfers between devices, exchange(): return (big, lax.ppermute(small, AXES, rotated(small_hops)))  22.9 us
    pallas_call x4, Pallas kernels, body(): advance(rotation, step[None], u, scale, *streamed, pair, big, small, firs...  19.2 us
    ppermute x4, starting transfers between devices, body(): second = lax.ppermute(second, AXES, SWAP_SECOND)  18.8 us
    ppermute x4, starting transfers between devices, exchange(): big = lax.ppermute(big, AXES, rotated(big_hops))  18.2 us
    ppermute x4, starting transfers between devices, exchange(): return (big, lax.ppermute(small, AXES, rotated(small_hops)))  15.2 us
    pallas_call x1, Pallas kernels, local(): pl.pallas_call(first_kernel, out_shape=sends, in_specs=[smem] + [hbm] * 4...  5.75 us
    another operation x1, loops' own time, local(): return lax.fori_loop(0, STEPS, body, tuple(carry))[0][None]  2.48 us
  transfers between devices with their start and end apart: 20, of which 5 were waited for; matrix products, arithmetic and copies ran while one was open for 2% of the time, Pallas kernels for 0%

commit v1 on v0

--- a/solution.py
+++ b/solution.py
@@ -160,8 +160,8 @@
 def copy_and_correct_edges(place, scale, edges, u_in, u):
     lane = lanes()
     first, second = [edge[...] for edge in edges]
-    high = jnp.where(place.even, first, second)
-    low = jnp.where(place.even, second, first)
+    high = jnp.where(place.even, second, first)
+    low = jnp.where(place.even, first, second)
     for a in range(N):
         for r in range(N):
             at = a * N + r
@@ -269,8 +269,8 @@
 
     zero = jnp.zeros((8, 128), jnp.float32)
     high, low = lax.fori_loop(0, N, column, (zero, zero))
-    edge_first[...] = jnp.where(where.even, high, low)
-    edge_second[...] = jnp.where(where.even, low, high)
+    edge_first[...] = jnp.where(where.even, low, high)
+    edge_second[...] = jnp.where(where.even, high, low)
     for a in range(N):
         for c in range(N):
             below = jnp.where(row == 0, 0.0, pltpu.roll(acc[a, 6, c], 1, 0))
@@ -504,8 +504,8 @@
     def body(step, carry):
         u, pair, big, small, first, second, scale, branch = carry
         pair = lax.ppermute(pair, AXES, PAIR)
-        first = lax.ppermute(first, AXES, SWAP_FIRST)
-        second = lax.ppermute(second, AXES, SWAP_SECOND)
+        first = lax.ppermute(first, AXES, SWAP_SECOND)
+        second = lax.ppermute(second, AXES, SWAP_FIRST)
         big, small = lax.switch(branch[0, 0], branches, big, small)
         streamed = [pltpu.with_memory_space_constraint(x, pltpu.HBM) for x in (coeffs, reaction)]
         return advance(

time: 106 us -> 107 us (level); the launches traced: 108 us -> 107 us
    ppermute x8, starting transfers between devices: 18.9 us -> 14.7 us  [the longest x4 12.7 us: body(): first = lax.ppermute(first, AXES, SWAP_SECOND)]
    ppermute x4, starting transfers between devices: 15.2 us -> 18.6 us  [exchange(): return (big, lax.ppermute(small, AXES, rotated(small_hops)))]
  transfers between devices with their start and end apart: 20 -> 20, of which waited for: 5 -> 4; matrix products, arithmetic and copies ran while one was open for 2% -> 2% of each run, Pallas kernels for 0% -> 0%
where the time goes in v1:
time: 107 us
  starting transfers between devices  52.8 us (49%)
  Pallas kernels  24.8 us (23%)
  waiting for transfers between devices  23.5 us (22%)
  local copies, waits for them, and re-layouts  3.11 us (3%)
  loops' own time  2.7 us (3%)
    ppermute x4, waiting for transfers between devices, exchange(): return (big, lax.ppermute(small, AXES, rotated(small_hops)))  23.5 us
    pallas_call x4, Pallas kernels, body(): advance(rotation, step[None], u, scale, *streamed, pair, big, small, firs...  19.1 us
    ppermute x4, starting transfers between devices, exchange(): return (big, lax.ppermute(small, AXES, rotated(small_hops)))  18.6 us
    ppermute x4, starting transfers between devices, exchange(): big = lax.ppermute(big, AXES, rotated(big_hops))  18.1 us
    ppermute x4, starting transfers between devices, body(): first = lax.ppermute(first, AXES, SWAP_SECOND)  12.7 us
    pallas_call x1, Pallas kernels, local(): pl.pallas_call(first_kernel, out_shape=sends, in_specs=[smem] + [hbm] * 4...  5.69 us
    another operation x1, loops' own time, local(): return lax.fori_loop(0, STEPS, body, tuple(carry))[0][None]  2.5 us
  transfers between devices with their start and end apart: 20, of which 4 were waited for; matrix products, arithmetic and copies ran while one was open for 2% of the time, Pallas kernels for 0%

profile of v1, /device:TPU:1, one launch (start us, length us, event | category | flops | bytes accessed | tf_op | source)
XLA Modules:
  0.0 107.0 jit_solution(7701471546844070530)
XLA Ops:
  0.0 5.7 %first.1 = (f32[7,7,7,8,128]{4,3,2,1,0:T(8,128)S(1)}, f32[7,7,8,128]{3,2,1,0:T(8,128)S(1)}, f32[49,8,128]{2,1,0:T(8,128)S(1)}, f32[25,8,128]{2,1,0:T(8,128)S(1)}...) custom-call(s32[4]{0:T(128)} %rotation.1, ...), custom_call_target="tpu_custom_call" | custom-call | tf_op jit(solution)/shard_map/first/pallas_call | solution.py:482
  5.7 100.2 %while.27 = (s32[]{:T(128)}, f32[7,7,7,8,128]{4,3,2,1,0:T(8,128)S(1)}, f32[7,7,8,128]{3,2,1,0:T(8,128)S(1)}, f32[49,8,128]{2,1,0:T(8,128)S(1)}, f32[25,8,128]{2,...) while((s32[]{:T(128)}, ...), condition=%wide.region_65.0_spmd, body=%wide.region_0.0_spmd.sunk | while | flops 3 | bytes 2048405 | solution.py:515
  8.7 7.2 %collective-permute-start.129 = (f32[8,128]{1,0:T(8,128)S(1)}, f32[8,128]{1,0:T(8,128)S(1)}, u32[]{:S(2)}, u32[]{:S(2)}) collective-permute-start(f32[8,128]{1,0:T(8,128)S(1)} %get-tuple-element.884), channel_id=1, source_target_pairs={{0,124},{1,125},{2,126},{3,127},{4,8},{5,9},{6,10},{7,11},{8,4},{9... | collective-permute-start | bytes 12296 | tf_op jit(solution)/shard_map/while/body/eval_jaxpr/ppermute | solution.py:507
  16.9 15.0 %conditional.2 = (f32[49,8,128]{2,1,0:T(8,128)}, f32[25,8,128]{2,1,0:T(8,128)}) conditional(s32[]{:T(128)} %bitcast.10, (f32[49,8,128]{2,1,0:T(8,128)S(1)}, f32[25,8,128]{2,1,0:T(8,128)S(1)}) %tuple.285, (f32[49,8,128]{2,1,0:T(8,128)S(1)}, f32[25,8,128]{2,1,0:T(8,128)S(1)}) %tuple.285, (f32[49,8,128]{2,1,0:T(8,128)S(1)}, ...), branch_computations={%region_1.0_spmd, %region_2.0_spmd, %region_3.0_spmd, %region_4.0_... | conditional | bytes 1212512 | solution.py:509
  17.0 3.1 %collective-permute-start.58 = (f32[49,8,128]{2,1,0:T(8,128)S(1)}, f32[49,8,128]{2,1,0:T(8,128)}, u32[]{:S(2)}, u32[]{:S(2)}) collective-permute-start(f32[49,8,128]{2,1,0:T(8,128)S(1)} %get-tuple-element.508), channel_id=1, source_target_pairs={{1,118},{2,13},{5,122},{6,17},{9,126},{10,21},{13,2},{14,25},{17,6... | collective-permute-start | bytes 602120 | tf_op jit(solution)/shard_map/while/body/eval_jaxpr/cond/branch_29_fun/ppermute | solution.py:458
  20.1 2.8 %collective-permute-start.59 = (f32[25,8,128]{2,1,0:T(8,128)S(1)}, f32[25,8,128]{2,1,0:T(8,128)}, u32[]{:S(2)}, u32[]{:S(2)}) collective-permute-start(f32[25,8,128]{2,1,0:T(8,128)S(1)} %get-tuple-element.509), channel_id=1, source_target_pairs={{1,122},{2,9},{5,126},{6,13},{9,2},{10,17},{13,6},{14,21},{17,10},... | collective-permute-start | bytes 307208 | tf_op jit(solution)/shard_map/while/body/eval_jaxpr/cond/branch_29_fun/ppermute | solution.py:459
  22.9 9.0 %collective-permute-done.59 = f32[25,8,128]{2,1,0:T(8,128)} collective-permute-done((f32[25,8,128]{2,1,0:T(8,128)S(1)}, f32[25,8,128]{2,1,0:T(8,128)}, u32[]{:S(2)}, u32[]{:S(2)}) %collective-permute-start.59) | collective-permute-done | bytes 102432 | tf_op jit(solution)/shard_map/while/body/eval_jaxpr/cond/branch_29_fun/ppermute | solution.py:459
  31.9 5.5 %step.5 = (f32[7,7,7,8,128]{4,3,2,1,0:T(8,128)S(1)}, f32[7,7,8,128]{3,2,1,0:T(8,128)S(1)}, f32[49,8,128]{2,1,0:T(8,128)S(1)}, f32[25,8,128]{2,1,0:T(8,128)S(1)},...) custom-call(s32[4]{0:T(128)S(1)} %get-tuple-element.903.rotation, ...), custom_call_target="tpu_custom_call", output_to_operand_aliasing={{0}: (2, {}), {6}: (3, {})} | custom-call | tf_op jit(solution)/shard_map/while/body/eval_jaxpr/step/pallas_call | solution.py:511
  39.4 17.2 %conditional.2 = (f32[49,8,128]{2,1,0:T(8,128)}, f32[25,8,128]{2,1,0:T(8,128)}) conditional(s32[]{:T(128)} %bitcast.10, (f32[49,8,128]{2,1,0:T(8,128)S(1)}, f32[25,8,128]{2,1,0:T(8,128)S(1)}) %tuple.285, (f32[49,8,128]{2,1,0:T(8,128)S(1)}, f32[25,8,128]{2,1,0:T(8,128)S(1)}) %tuple.285, (f32[49,8,128]{2,1,0:T(8,128)S(1)}, ...), branch_computations={%region_1.0_spmd, %region_2.0_spmd, %region_3.0_spmd, %region_4.0_... | conditional | bytes 1212512 | solution.py:509
  39.4 5.3 %collective-permute-start.124 = (f32[49,8,128]{2,1,0:T(8,128)S(1)}, f32[49,8,128]{2,1,0:T(8,128)}, u32[]{:S(2)}, u32[]{:S(2)}) collective-permute-start(f32[49,8,128]{2,1,0:T(8,128)S(1)} %get-tuple-element.574), channel_id=1, source_target_pairs={{1,126},{2,5},{5,2},{6,9},{9,6},{10,13},{13,10},{14,17},{17,14},{1... | collective-permute-start | bytes 602120 | tf_op jit(solution)/shard_map/while/body/eval_jaxpr/cond/branch_62_fun/ppermute | solution.py:458
  44.7 6.6 %collective-permute-start.125 = (f32[25,8,128]{2,1,0:T(8,128)S(1)}, f32[25,8,128]{2,1,0:T(8,128)}, u32[]{:S(2)}, u32[]{:S(2)}) collective-permute-start(f32[25,8,128]{2,1,0:T(8,128)S(1)} %get-tuple-element.575), channel_id=1, source_target_pairs={{1,122},{2,9},{5,126},{6,13},{9,2},{10,17},{13,6},{14,21},{17,10},... | collective-permute-start | bytes 307208 | tf_op jit(solution)/shard_map/while/body/eval_jaxpr/cond/branch_62_fun/ppermute | solution.py:459
  51.3 5.2 %collective-permute-done.125 = f32[25,8,128]{2,1,0:T(8,128)} collective-permute-done((f32[25,8,128]{2,1,0:T(8,128)S(1)}, f32[25,8,128]{2,1,0:T(8,128)}, u32[]{:S(2)}, u32[]{:S(2)}) %collective-permute-start.125) | collective-permute-done | bytes 102432 | tf_op jit(solution)/shard_map/while/body/eval_jaxpr/cond/branch_62_fun/ppermute | solution.py:459
  56.6 5.6 %step.5 = (f32[7,7,7,8,128]{4,3,2,1,0:T(8,128)S(1)}, f32[7,7,8,128]{3,2,1,0:T(8,128)S(1)}, f32[49,8,128]{2,1,0:T(8,128)S(1)}, f32[25,8,128]{2,1,0:T(8,128)S(1)},...) custom-call(s32[4]{0:T(128)S(1)} %get-tuple-element.903.rotation, ...), custom_call_target="tpu_custom_call", output_to_operand_aliasing={{0}: (2, {}), {6}: (3, {})} | custom-call | tf_op jit(solution)/shard_map/while/body/eval_jaxpr/step/pallas_call | solution.py:511
  63.5 14.7 %conditional.2 = (f32[49,8,128]{2,1,0:T(8,128)}, f32[25,8,128]{2,1,0:T(8,128)}) conditional(s32[]{:T(128)} %bitcast.10, (f32[49,8,128]{2,1,0:T(8,128)S(1)}, f32[25,8,128]{2,1,0:T(8,128)S(1)}) %tuple.285, (f32[49,8,128]{2,1,0:T(8,128)S(1)}, f32[25,8,128]{2,1,0:T(8,128)S(1)}) %tuple.285, (f32[49,8,128]{2,1,0:T(8,128)S(1)}, ...), branch_computations={%region_1.0_spmd, %region_2.0_spmd, %region_3.0_spmd, %region_4.0_... | conditional | bytes 1212512 | solution.py:509
  63.5 7.7 %collective-permute-start = (f32[49,8,128]{2,1,0:T(8,128)S(1)}, f32[49,8,128]{2,1,0:T(8,128)}, u32[]{:S(2)}, u32[]{:S(2)}) collective-permute-start(f32[49,8,128]{2,1,0:T(8,128)S(1)} %get-tuple-element.450), channel_id=1, source_target_pairs={{1,2},{2,1},{5,6},{6,5},{9,10},{10,9},{13,14},{14,13},{17,18},{18,... | collective-permute-start | bytes 602120 | tf_op jit(solution)/shard_map/while/body/eval_jaxpr/cond/branch_0_fun/ppermute | solution.py:458
  71.3 1.9 %collective-permute-start.1 = (f32[25,8,128]{2,1,0:T(8,128)S(1)}, f32[25,8,128]{2,1,0:T(8,128)}, u32[]{:S(2)}, u32[]{:S(2)}) collective-permute-start(f32[25,8,128]{2,1,0:T(8,128)S(1)} %get-tuple-element.451), channel_id=1, source_target_pairs={{1,6},{2,125},{5,10},{6,1},{9,14},{10,5},{13,18},{14,9},{17,22},{1... | collective-permute-start | bytes 307208 | tf_op jit(solution)/shard_map/while/body/eval_jaxpr/cond/branch_0_fun/ppermute | solution.py:459
  73.2 5.1 %collective-permute-done.1 = f32[25,8,128]{2,1,0:T(8,128)} collective-permute-done((f32[25,8,128]{2,1,0:T(8,128)S(1)}, f32[25,8,128]{2,1,0:T(8,128)}, u32[]{:S(2)}, u32[]{:S(2)}) %collective-permute-start.1) | collective-permute-done | bytes 102432 | tf_op jit(solution)/shard_map/while/body/eval_jaxpr/cond/branch_0_fun/ppermute | solution.py:459
  78.3 5.5 %step.5 = (f32[7,7,7,8,128]{4,3,2,1,0:T(8,128)S(1)}, f32[7,7,8,128]{3,2,1,0:T(8,128)S(1)}, f32[49,8,128]{2,1,0:T(8,128)S(1)}, f32[25,8,128]{2,1,0:T(8,128)S(1)},...) custom-call(s32[4]{0:T(128)S(1)} %get-tuple-element.903.rotation, ...), custom_call_target="tpu_custom_call", output_to_operand_aliasing={{0}: (2, {}), {6}: (3, {})} | custom-call | tf_op jit(solution)/shard_map/while/body/eval_jaxpr/step/pallas_call | solution.py:511
  84.0 4.8 %collective-permute-start.129 = (f32[8,128]{1,0:T(8,128)S(1)}, f32[8,128]{1,0:T(8,128)S(1)}, u32[]{:S(2)}, u32[]{:S(2)}) collective-permute-start(f32[8,128]{1,0:T(8,128)S(1)} %get-tuple-element.884), channel_id=1, source_target_pairs={{0,124},{1,125},{2,126},{3,127},{4,8},{5,9},{6,10},{7,11},{8,4},{9... | collective-permute-start | bytes 12296 | tf_op jit(solution)/shard_map/while/body/eval_jaxpr/ppermute | solution.py:507
  89.9 13.5 %conditional.2 = (f32[49,8,128]{2,1,0:T(8,128)}, f32[25,8,128]{2,1,0:T(8,128)}) conditional(s32[]{:T(128)} %bitcast.10, (f32[49,8,128]{2,1,0:T(8,128)S(1)}, f32[25,8,128]{2,1,0:T(8,128)S(1)}) %tuple.285, (f32[49,8,128]{2,1,0:T(8,128)S(1)}, f32[25,8,128]{2,1,0:T(8,128)S(1)}) %tuple.285, (f32[49,8,128]{2,1,0:T(8,128)S(1)}, ...), branch_computations={%region_1.0_spmd, %region_2.0_spmd, %region_3.0_spmd, %region_4.0_... | conditional | bytes 1212512 | solution.py:509
  89.9 1.9 %collective-permute-start.126 = (f32[49,8,128]{2,1,0:T(8,128)S(1)}, f32[49,8,128]{2,1,0:T(8,128)}, u32[]{:S(2)}, u32[]{:S(2)}) collective-permute-start(f32[49,8,128]{2,1,0:T(8,128)S(1)} %get-tuple-element.576), channel_id=1, source_target_pairs={{1,2},{2,1},{5,6},{6,5},{9,10},{10,9},{13,14},{14,13},{17,18},{18,... | collective-permute-start | bytes 602120 | tf_op jit(solution)/shard_map/while/body/eval_jaxpr/cond/branch_63_fun/ppermute | solution.py:458
  91.8 7.3 %collective-permute-start.127 = (f32[25,8,128]{2,1,0:T(8,128)S(1)}, f32[25,8,128]{2,1,0:T(8,128)}, u32[]{:S(2)}, u32[]{:S(2)}) collective-permute-start(f32[25,8,128]{2,1,0:T(8,128)S(1)} %get-tuple-element.577), channel_id=1, source_target_pairs={{1,126},{2,5},{5,2},{6,9},{9,6},{10,13},{13,10},{14,17},{17,14},{1... | collective-permute-start | bytes 307208 | tf_op jit(solution)/shard_map/while/body/eval_jaxpr/cond/branch_63_fun/ppermute | solution.py:459
  99.2 4.2 %collective-permute-done.127 = f32[25,8,128]{2,1,0:T(8,128)} collective-permute-done((f32[25,8,128]{2,1,0:T(8,128)S(1)}, f32[25,8,128]{2,1,0:T(8,128)}, u32[]{:S(2)}, u32[]{:S(2)}) %collective-permute-start.127) | collective-permute-done | bytes 102432 | tf_op jit(solution)/shard_map/while/body/eval_jaxpr/cond/branch_63_fun/ppermute | solution.py:459
  103.4 2.5 %step.5 = (f32[7,7,7,8,128]{4,3,2,1,0:T(8,128)S(1)}, f32[7,7,8,128]{3,2,1,0:T(8,128)S(1)}, f32[49,8,128]{2,1,0:T(8,128)S(1)}, f32[25,8,128]{2,1,0:T(8,128)S(1)},...) custom-call(s32[4]{0:T(128)S(1)} %get-tuple-element.903.rotation, ...), custom_call_target="tpu_custom_call", output_to_operand_aliasing={{0}: (2, {}), {6}: (3, {})} | custom-call | tf_op jit(solution)/shard_map/while/body/eval_jaxpr/step/pallas_call | solution.py:511
  (33 shorter events, 7.4 us)
Async XLA Ops:
  0.0 5.7 %copy-start = (s32[4]{0:T(128)S(1)}, s32[4]{0:T(128)}, u32[]{:S(2)}) copy-start(s32[4]{0:T(128)} %rotation.1) | copy-start | bytes 52
  5.7 26.2 %collective-permute-start.128 = (f32[7,7,8,128]{3,2,1,0:T(8,128)S(1)}, f32[7,7,8,128]{3,2,1,0:T(8,128)S(1)}, u32[]{:S(2)}, u32[]{:S(2)}) collective-permute-start(f32[7,7,8,128]{3,2,1,0:T(8,128)S(1)} %get-tuple-element.881), channel_id=1, source_target_pairs={{0,1},{1,0},{2,3},{3,2},{4,5},{5,4},{6,7},{7,6},{8,9},{9,8},{10,11... | collective-permute-start | bytes 602120 | tf_op jit(solution)/shard_map/while/body/eval_jaxpr/ppermute | solution.py:506
  6.9 25.0 %collective-permute-start.130 = (f32[8,128]{1,0:T(8,128)S(1)}, f32[8,128]{1,0:T(8,128)S(1)}, u32[]{:S(2)}, u32[]{:S(2)}) collective-permute-start(f32[8,128]{1,0:T(8,128)S(1)} %get-tuple-element.885), channel_id=1, source_target_pairs={{0,4},{1,5},{2,6},{3,7},{4,0},{5,1},{6,2},{7,3},{8,12},{9,13},{10,... | collective-permute-start | bytes 12296 | tf_op jit(solution)/shard_map/while/body/eval_jaxpr/ppermute | solution.py:508
  8.7 23.2 %collective-permute-start.129 = (f32[8,128]{1,0:T(8,128)S(1)}, f32[8,128]{1,0:T(8,128)S(1)}, u32[]{:S(2)}, u32[]{:S(2)}) collective-permute-start(f32[8,128]{1,0:T(8,128)S(1)} %get-tuple-element.884), channel_id=1, source_target_pairs={{0,124},{1,125},{2,126},{3,127},{4,8},{5,9},{6,10},{7,11},{8,4},{9... | collective-permute-start | bytes 12296 | tf_op jit(solution)/shard_map/while/body/eval_jaxpr/ppermute | solution.py:507
  17.0 14.9 %collective-permute-start.58 = (f32[49,8,128]{2,1,0:T(8,128)S(1)}, f32[49,8,128]{2,1,0:T(8,128)}, u32[]{:S(2)}, u32[]{:S(2)}) collective-permute-start(f32[49,8,128]{2,1,0:T(8,128)S(1)} %get-tuple-element.508), channel_id=1, source_target_pairs={{1,118},{2,13},{5,122},{6,17},{9,126},{10,21},{13,2},{14,25},{17,6... | collective-permute-start | bytes 602120 | tf_op jit(solution)/shard_map/while/body/eval_jaxpr/cond/branch_29_fun/ppermute | solution.py:458
  20.1 11.8 %collective-permute-start.59 = (f32[25,8,128]{2,1,0:T(8,128)S(1)}, f32[25,8,128]{2,1,0:T(8,128)}, u32[]{:S(2)}, u32[]{:S(2)}) collective-permute-start(f32[25,8,128]{2,1,0:T(8,128)S(1)} %get-tuple-element.509), channel_id=1, source_target_pairs={{1,122},{2,9},{5,126},{6,13},{9,2},{10,17},{13,6},{14,21},{17,10},... | collective-permute-start | bytes 307208 | tf_op jit(solution)/shard_map/while/body/eval_jaxpr/cond/branch_29_fun/ppermute | solution.py:459
  37.5 19.1 %collective-permute-start.128 = (f32[7,7,8,128]{3,2,1,0:T(8,128)S(1)}, f32[7,7,8,128]{3,2,1,0:T(8,128)S(1)}, u32[]{:S(2)}, u32[]{:S(2)}) collective-permute-start(f32[7,7,8,128]{3,2,1,0:T(8,128)S(1)} %get-tuple-element.881), channel_id=1, source_target_pairs={{0,1},{1,0},{2,3},{3,2},{4,5},{5,4},{6,7},{7,6},{8,9},{9,8},{10,11... | collective-permute-start | bytes 602120 | tf_op jit(solution)/shard_map/while/body/eval_jaxpr/ppermute | solution.py:506
  37.6 19.0 %collective-permute-start.130 = (f32[8,128]{1,0:T(8,128)S(1)}, f32[8,128]{1,0:T(8,128)S(1)}, u32[]{:S(2)}, u32[]{:S(2)}) collective-permute-start(f32[8,128]{1,0:T(8,128)S(1)} %get-tuple-element.885), channel_id=1, source_target_pairs={{0,4},{1,5},{2,6},{3,7},{4,0},{5,1},{6,2},{7,3},{8,12},{9,13},{10,... | collective-permute-start | bytes 12296 | tf_op jit(solution)/shard_map/while/body/eval_jaxpr/ppermute | solution.py:508
  37.7 18.9 %collective-permute-start.129 = (f32[8,128]{1,0:T(8,128)S(1)}, f32[8,128]{1,0:T(8,128)S(1)}, u32[]{:S(2)}, u32[]{:S(2)}) collective-permute-start(f32[8,128]{1,0:T(8,128)S(1)} %get-tuple-element.884), channel_id=1, source_target_pairs={{0,124},{1,125},{2,126},{3,127},{4,8},{5,9},{6,10},{7,11},{8,4},{9... | collective-permute-start | bytes 12296 | tf_op jit(solution)/shard_map/while/body/eval_jaxpr/ppermute | solution.py:507
  39.4 17.1 %collective-permute-start.124 = (f32[49,8,128]{2,1,0:T(8,128)S(1)}, f32[49,8,128]{2,1,0:T(8,128)}, u32[]{:S(2)}, u32[]{:S(2)}) collective-permute-start(f32[49,8,128]{2,1,0:T(8,128)S(1)} %get-tuple-element.574), channel_id=1, source_target_pairs={{1,126},{2,5},{5,2},{6,9},{9,6},{10,13},{13,10},{14,17},{17,14},{1... | collective-permute-start | bytes 602120 | tf_op jit(solution)/shard_map/while/body/eval_jaxpr/cond/branch_62_fun/ppermute | solution.py:458
  44.7 11.8 %collective-permute-start.125 = (f32[25,8,128]{2,1,0:T(8,128)S(1)}, f32[25,8,128]{2,1,0:T(8,128)}, u32[]{:S(2)}, u32[]{:S(2)}) collective-permute-start(f32[25,8,128]{2,1,0:T(8,128)S(1)} %get-tuple-element.575), channel_id=1, source_target_pairs={{1,122},{2,9},{5,126},{6,13},{9,2},{10,17},{13,6},{14,21},{17,10},... | collective-permute-start | bytes 307208 | tf_op jit(solution)/shard_map/while/body/eval_jaxpr/cond/branch_62_fun/ppermute | solution.py:459
  62.2 16.1 %collective-permute-start.128 = (f32[7,7,8,128]{3,2,1,0:T(8,128)S(1)}, f32[7,7,8,128]{3,2,1,0:T(8,128)S(1)}, u32[]{:S(2)}, u32[]{:S(2)}) collective-permute-start(f32[7,7,8,128]{3,2,1,0:T(8,128)S(1)} %get-tuple-element.881), channel_id=1, source_target_pairs={{0,1},{1,0},{2,3},{3,2},{4,5},{5,4},{6,7},{7,6},{8,9},{9,8},{10,11... | collective-permute-start | bytes 602120 | tf_op jit(solution)/shard_map/while/body/eval_jaxpr/ppermute | solution.py:506
  62.3 16.0 %collective-permute-start.130 = (f32[8,128]{1,0:T(8,128)S(1)}, f32[8,128]{1,0:T(8,128)S(1)}, u32[]{:S(2)}, u32[]{:S(2)}) collective-permute-start(f32[8,128]{1,0:T(8,128)S(1)} %get-tuple-element.885), channel_id=1, source_target_pairs={{0,4},{1,5},{2,6},{3,7},{4,0},{5,1},{6,2},{7,3},{8,12},{9,13},{10,... | collective-permute-start | bytes 12296 | tf_op jit(solution)/shard_map/while/body/eval_jaxpr/ppermute | solution.py:508
  62.4 15.9 %collective-permute-start.129 = (f32[8,128]{1,0:T(8,128)S(1)}, f32[8,128]{1,0:T(8,128)S(1)}, u32[]{:S(2)}, u32[]{:S(2)}) collective-permute-start(f32[8,128]{1,0:T(8,128)S(1)} %get-tuple-element.884), channel_id=1, source_target_pairs={{0,124},{1,125},{2,126},{3,127},{4,8},{5,9},{6,10},{7,11},{8,4},{9... | collective-permute-start | bytes 12296 | tf_op jit(solution)/shard_map/while/body/eval_jaxpr/ppermute | solution.py:507
  63.5 14.7 %collective-permute-start = (f32[49,8,128]{2,1,0:T(8,128)S(1)}, f32[49,8,128]{2,1,0:T(8,128)}, u32[]{:S(2)}, u32[]{:S(2)}) collective-permute-start(f32[49,8,128]{2,1,0:T(8,128)S(1)} %get-tuple-element.450), channel_id=1, source_target_pairs={{1,2},{2,1},{5,6},{6,5},{9,10},{10,9},{13,14},{14,13},{17,18},{18,... | collective-permute-start | bytes 602120 | tf_op jit(solution)/shard_map/while/body/eval_jaxpr/cond/branch_0_fun/ppermute | solution.py:458
  71.3 7.0 %collective-permute-start.1 = (f32[25,8,128]{2,1,0:T(8,128)S(1)}, f32[25,8,128]{2,1,0:T(8,128)}, u32[]{:S(2)}, u32[]{:S(2)}) collective-permute-start(f32[25,8,128]{2,1,0:T(8,128)S(1)} %get-tuple-element.451), channel_id=1, source_target_pairs={{1,6},{2,125},{5,10},{6,1},{9,14},{10,5},{13,18},{14,9},{17,22},{1... | collective-permute-start | bytes 307208 | tf_op jit(solution)/shard_map/while/body/eval_jaxpr/cond/branch_0_fun/ppermute | solution.py:459
  83.8 19.5 %collective-permute-start.128 = (f32[7,7,8,128]{3,2,1,0:T(8,128)S(1)}, f32[7,7,8,128]{3,2,1,0:T(8,128)S(1)}, u32[]{:S(2)}, u32[]{:S(2)}) collective-permute-start(f32[7,7,8,128]{3,2,1,0:T(8,128)S(1)} %get-tuple-element.881), channel_id=1, source_target_pairs={{0,1},{1,0},{2,3},{3,2},{4,5},{5,4},{6,7},{7,6},{8,9},{9,8},{10,11... | collective-permute-start | bytes 602120 | tf_op jit(solution)/shard_map/while/body/eval_jaxpr/ppermute | solution.py:506
  83.9 19.4 %collective-permute-start.130 = (f32[8,128]{1,0:T(8,128)S(1)}, f32[8,128]{1,0:T(8,128)S(1)}, u32[]{:S(2)}, u32[]{:S(2)}) collective-permute-start(f32[8,128]{1,0:T(8,128)S(1)} %get-tuple-element.885), channel_id=1, source_target_pairs={{0,4},{1,5},{2,6},{3,7},{4,0},{5,1},{6,2},{7,3},{8,12},{9,13},{10,... | collective-permute-start | bytes 12296 | tf_op jit(solution)/shard_map/while/body/eval_jaxpr/ppermute | solution.py:508
  84.0 19.3 %collective-permute-start.129 = (f32[8,128]{1,0:T(8,128)S(1)}, f32[8,128]{1,0:T(8,128)S(1)}, u32[]{:S(2)}, u32[]{:S(2)}) collective-permute-start(f32[8,128]{1,0:T(8,128)S(1)} %get-tuple-element.884), channel_id=1, source_target_pairs={{0,124},{1,125},{2,126},{3,127},{4,8},{5,9},{6,10},{7,11},{8,4},{9... | collective-permute-start | bytes 12296 | tf_op jit(solution)/shard_map/while/body/eval_jaxpr/ppermute | solution.py:507
  89.9 13.4 %collective-permute-start.126 = (f32[49,8,128]{2,1,0:T(8,128)S(1)}, f32[49,8,128]{2,1,0:T(8,128)}, u32[]{:S(2)}, u32[]{:S(2)}) collective-permute-start(f32[49,8,128]{2,1,0:T(8,128)S(1)} %get-tuple-element.576), channel_id=1, source_target_pairs={{1,2},{2,1},{5,6},{6,5},{9,10},{10,9},{13,14},{14,13},{17,18},{18,... | collective-permute-start | bytes 602120 | tf_op jit(solution)/shard_map/while/body/eval_jaxpr/cond/branch_63_fun/ppermute | solution.py:458
  91.8 11.5 %collective-permute-start.127 = (f32[25,8,128]{2,1,0:T(8,128)S(1)}, f32[25,8,128]{2,1,0:T(8,128)}, u32[]{:S(2)}, u32[]{:S(2)}) collective-permute-start(f32[25,8,128]{2,1,0:T(8,128)S(1)} %get-tuple-element.577), channel_id=1, source_target_pairs={{1,126},{2,5},{5,2},{6,9},{9,6},{10,13},{13,10},{14,17},{17,14},{1... | collective-permute-start | bytes 307208 | tf_op jit(solution)/shard_map/while/body/eval_jaxpr/cond/branch_63_fun/ppermute | solution.py:459
